TPU v7x, 16 devices: a whole 2x2x2 slice. The times are simulated.
16 devices in a mesh: dp: 4 (over z, y), tp: 4 (over x, core).
Axes of the slice: x: 2, y: 2, z: 2, core: 2. Of those that a mesh axis runs over, the one named last changes fastest.
Arguments:
- hidden: bfloat16 [512, 4096], P('dp'), parts along dimension 0
- positions: int32 [512], P('dp'), parts along dimension 0
- k_cache: bfloat16 [2, 512, 64, 8, 128], P(None, 'dp', None, 'tp'), parts along dimension 1
- v_cache: bfloat16 [2, 512, 64, 8, 128], P(None, 'dp', None, 'tp'), parts along dimension 1
- attn_norm: bfloat16 [2, 4096], replicated
- w_query: bfloat16 [2, 4096, 4096], P(None, None, 'tp')
- w_key: bfloat16 [2, 4096, 1024], P(None, None, 'tp')
- w_value: bfloat16 [2, 4096, 1024], P(None, None, 'tp')
- w_out: bfloat16 [2, 4096, 4096], P(None, 'tp')
- mlp_norm: bfloat16 [2, 4096], replicated
- w_gate: bfloat16 [2, 4096, 14336], P(None, None, 'tp')
- w_up: bfloat16 [2, 4096, 14336], P(None, None, 'tp')
- w_down: bfloat16 [2, 14336, 4096], P(None, 'tp')
Outputs:
- output 1: bfloat16 [512, 4096], P('dp'), parts along dimension 0
- output 2: bfloat16 [2, 512, 64, 8, 128], P(None, 'dp', None, 'tp'), parts along dimension 1
- output 3: bfloat16 [2, 512, 64, 8, 128], P(None, 'dp', None, 'tp'), parts along dimension 1
There are 4 independent parts. A program takes and returns all parts, laid end to end along the dimension named above; an argument that names none is the same for every part.
All inputs are finite; a program needn't handle non-finite values.
Results may differ from a plain program's by a relative error of at most 0.02.
Values are sent between devices in bfloat16 or wider.
A program may use at most 1 GiB of HBM per device.

v0:
```python
import math
import jax
import jax.numpy as jnp
from jax import lax
from jax.sharding import PartitionSpec as P


def rms_norm(hidden, weight):
    hidden_f32 = hidden.astype(jnp.float32)
    mean_sq = jnp.mean(hidden_f32 * hidden_f32, axis=-1, keepdims=True)
    return (hidden_f32 * lax.rsqrt(mean_sq + 1e-5) * weight.astype(jnp.float32)).astype(jnp.bfloat16)


def rope_tables(positions, head_dim):
    half_dim = head_dim // 2
    inv_freq = jnp.power(500000.0, -jnp.arange(half_dim, dtype=jnp.float32) * (2.0 / head_dim))
    wavelen = (2.0 * math.pi) / inv_freq
    smooth = (8192.0 / wavelen - 1.0) / 3.0
    blended = (1.0 - smooth) * inv_freq / 8.0 + smooth * inv_freq
    scaled = jnp.where(wavelen < 2048.0, inv_freq, jnp.where(wavelen > 8192.0, inv_freq / 8.0, blended))
    angles = positions.astype(jnp.float32)[:, None] * scaled[None, :]
    return jnp.cos(angles), jnp.sin(angles)


def apply_rope(vectors, cos_tab, sin_tab):
    half_dim = vectors.shape[-1] // 2
    vec_f32 = vectors.astype(jnp.float32)
    first = vec_f32[..., :half_dim]
    second = vec_f32[..., half_dim:]
    cos_b = cos_tab[:, None, :]
    sin_b = sin_tab[:, None, :]
    return jnp.concatenate([first * cos_b - second * sin_b, second * cos_b + first * sin_b], axis=-1).astype(jnp.bfloat16)


def attend_split(query, k_old, v_old, key_new, value_new, before):
    score_scale = query.shape[-1] ** -0.5
    scores = jnp.einsum('bkgd,bskd->bkgs', query, k_old, preferred_element_type=jnp.float32) * score_scale
    scores = jnp.where(before, scores, -jnp.inf)
    score_new = jnp.einsum('clhe,cle->clh', query, key_new, preferred_element_type=jnp.float32) * score_scale
    row_peak = jnp.maximum(jnp.max(scores, axis=-1), score_new)
    weight_old = jnp.exp(scores - row_peak[..., None])
    weight_new = jnp.exp(score_new - row_peak)
    inv_total = 1.0 / (jnp.sum(weight_old, axis=-1) + weight_new)
    prob_old = (weight_old * inv_total[..., None]).astype(jnp.bfloat16)
    prob_new = (weight_new * inv_total).astype(jnp.bfloat16)
    attn_out = jnp.einsum('bkgs,bskd->bkgd', prob_old, v_old, preferred_element_type=jnp.float32)
    attn_out = attn_out + prob_new[..., None].astype(jnp.float32) * value_new[:, :, None, :].astype(jnp.float32)
    return attn_out.astype(jnp.bfloat16)


def attention_block(hidden, norm_weight, wq_layer, wk_layer, wv_layer, wo_layer, k_old, v_old, cos_tab, sin_tab, before):
    batch_size = hidden.shape[0]
    kv_heads = k_old.shape[2]
    head_dim = k_old.shape[3]
    q_heads = wq_layer.shape[1] // head_dim
    normed = rms_norm(hidden, norm_weight)
    query = jnp.dot(normed, wq_layer, preferred_element_type=jnp.float32).astype(jnp.bfloat16)
    key_new = jnp.dot(normed, wk_layer, preferred_element_type=jnp.float32).astype(jnp.bfloat16)
    value_new = jnp.dot(normed, wv_layer, preferred_element_type=jnp.float32).astype(jnp.bfloat16)
    query = apply_rope(query.reshape(batch_size, q_heads, head_dim), cos_tab, sin_tab)
    key_new = apply_rope(key_new.reshape(batch_size, kv_heads, head_dim), cos_tab, sin_tab)
    value_new = value_new.reshape(batch_size, kv_heads, head_dim)
    attended = attend_split(query.reshape(batch_size, kv_heads, q_heads // kv_heads, head_dim), k_old, v_old, key_new, value_new, before)
    mixed = jnp.dot(attended.reshape(batch_size, q_heads * head_dim), wo_layer, preferred_element_type=jnp.float32)
    return mixed.astype(jnp.bfloat16), key_new, value_new


def mlp_block(hidden, norm_weight, wg_layer, wu_layer, wd_layer):
    normed = rms_norm(hidden, norm_weight)
    gate_proj = jnp.dot(normed, wg_layer, preferred_element_type=jnp.float32).astype(jnp.bfloat16)
    up_proj = jnp.dot(normed, wu_layer, preferred_element_type=jnp.float32).astype(jnp.bfloat16)
    activated = (jax.nn.silu(gate_proj.astype(jnp.float32)) * up_proj.astype(jnp.float32)).astype(jnp.bfloat16)
    return jnp.dot(activated, wd_layer, preferred_element_type=jnp.float32).astype(jnp.bfloat16)


def write_rows(cache, rows, positions):
    at_pos = (jnp.arange(cache.shape[2])[None, :] == positions[:, None])[None, :, :, None, None]
    return jnp.where(at_pos, rows[:, :, None], cache)


def solution(mesh):
    row_spec = P('dp', None)
    pos_spec = P('dp')
    cache_spec = P(None, 'dp', None, 'tp', None)
    norm_spec = P(None, None)
    col_spec = P(None, None, 'tp')
    split_rows = P(None, 'tp', None)

    def local_step(hidden, positions, k_cache, v_cache, attn_norm, w_query, w_key, w_value, w_out, mlp_norm, w_gate, w_up, w_down):
        cos_tab, sin_tab = rope_tables(positions, k_cache.shape[4])
        before = (jnp.arange(k_cache.shape[2])[None, :] < positions[:, None])[:, None, None, :]
        k_rows = []
        v_rows = []
        for layer in range(k_cache.shape[0]):
            part_out, key_new, value_new = attention_block(hidden, attn_norm[layer], w_query[layer], w_key[layer], w_value[layer], w_out[layer], k_cache[layer], v_cache[layer], cos_tab, sin_tab, before)
            hidden = hidden + lax.psum(part_out, 'tp')
            part_out = mlp_block(hidden, mlp_norm[layer], w_gate[layer], w_up[layer], w_down[layer])
            hidden = hidden + lax.psum(part_out, 'tp')
            k_rows.append(key_new)
            v_rows.append(value_new)
        k_out = write_rows(k_cache, jnp.stack(k_rows), positions)
        v_out = write_rows(v_cache, jnp.stack(v_rows), positions)
        return hidden, k_out, v_out

    return jax.shard_map(local_step, mesh=mesh, in_specs=(row_spec, pos_spec, cache_spec, cache_spec, norm_spec, col_spec, col_spec, col_spec, split_rows, norm_spec, col_spec, col_spec, split_rows), out_specs=(row_spec, cache_spec, cache_spec), check_vma=False)
```

profile of v0, /device:TPU:0, one launch (start us, length us, event | category | flops | bytes accessed | tf_op | source)
XLA Modules:
  0.0 300.1 jit_solution(14103704693545086291)
XLA Ops:
  7.2 0.7 convert_element_type.192
  7.9 0.7 iota_compare_fusion
  8.6 1.5 fusion.86
  10.2 0.8 slice_convert_fusion.1
  11.0 2.5 fusion.149
  13.6 2.1 fusion.161
  15.7 0.1 reshape.263
  15.8 4.7 %fusion.130 = f32[16,8,8,128]{3,1,2,0:T(8,128)S(1)} fusion(bf16[2,4096,1024]{2,1,0:T(8,128)(2,1)} %param.18, bf16[128,4096]{1,0:T(8,128)(2,1)S(1)} %copy-done, f32[4096]{0:T(1024)S(1)} %bitcast.213, f32[128]{0:T(128)S(1)} %add_rsqrt_fusion.3), kind=kOutput, calls=%fused_computation.104 | convolution fusion | flops 1076101120 | bytes 9978368 | tf_op jit(solution)/shard_map/dot_general | solution.py:57
  20.4 0.1 copy.52
  20.5 0.3 multiply_cosine_fusion
  20.9 0.3 subtract_convert_fusion.3
  21.1 0.3 subtract_convert_fusion.1
  21.4 0.2 maximum_bitcast_fusion
  21.6 0.5 fusion.180
  22.1 0.1 copy.45
  22.2 12.1 %fusion.194 = (bf16[1,128,64,2,128]{4,3,2,1,0:T(2,128)(2,1)}, bf16[1,128,64,2,128]{4,3,2,1,0:T(2,128)(2,1)S(1)}) fusion(bf16[2,128,64,2,128]{4,3,2,1,0:T(2,128)(2,1)} %param.15), kind=kLoop, calls=%fused_computation.176 | loop fusion | bytes 16777216 | tf_op jit(solution)/shard_map/slice | solution.py:95
  34.3 2.7 fusion.196
  37.0 0.1 copy.31
  37.1 0.2 copy.32
  37.3 0.8 fusion.166
  38.1 0.1 copy.33
  38.2 0.2 copy.34
  38.4 0.2 copy.36
  38.5 10.3 %fusion.195 = (bf16[1,128,64,2,128]{4,3,2,1,0:T(2,128)(2,1)}, bf16[1,128,64,2,128]{4,3,2,1,0:T(2,128)(2,1)S(1)}) fusion(bf16[2,128,64,2,128]{4,3,2,1,0:T(2,128)(2,1)} %param.16), kind=kLoop, calls=%fused_computation.177 | loop fusion | bytes 16777216 | tf_op jit(solution)/shard_map/slice | solution.py:95
  48.8 1.7 fusion.143
  50.5 0.2 reshape.259
  50.7 5.6 %fusion.30 = bf16[128,4096]{1,0:T(8,128)(2,1)} fusion(bf16[128,1024]{1,0:T(8,128)(2,1)S(1)} %reshape.259, bf16[2,1024,4096]{2,1,0:T(8,128)(2,1)} %param.21), kind=kOutput, calls=%fused_computation.32 | convolution fusion | flops 1074266112 | bytes 9699328 | tf_op jit(solution)/shard_map/dot_general | solution.py:64
  56.4 0.2 all-reduce.7.cloned.1.call-start
  56.6 35.3 %all-reduce.5.cloned.1.call-done = bf16[128,4096]{1,0:T(8,128)(2,1)} async-done(((bf16[128,4096]{1,0:T(8,128)(2,1)}), bf16[128,4096]{1,0:T(8,128)(2,1)}) %all-reduce.5.cloned.1.call-update) | async-done | bytes 1048592 | tf_op jit(solution)/shard_map/psum | solution.py:96
  92.0 1.7 fusion.89
  93.7 12.8 %fusion.39 = f32[128,3584]{1,0:T(8,128)} fusion(bf16[2,4096,3584]{2,1,0:T(8,128)(2,1)} %param.23, bf16[128,4096]{1,0:T(8,128)(2,1)S(1)} %get-tuple-element.8, f32[4096]{0:T(1024)S(1)} %bitcast.209, f32[128]{0:T(128)S(1)} %add_rsqrt_fusion.2), kind=kOutput, calls=%fused_computation.35 | convolution fusion | flops 3761111040 | bytes 32260608 | tf_op jit(solution)/shard_map/dot_general | solution.py:70
  106.4 22.1 %fusion.54 = bf16[128,4096]{1,0:T(8,128)(2,1)} fusion(bf16[2,3584,4096]{2,1,0:T(8,128)(2,1)} %param.25, bf16[2,4096,3584]{2,1,0:T(8,128)(2,1)} %param.24, f32[128,3584]{1,0:T(8,128)} %fusion.39, bf16[128,4096]{1,0:T(8,128)(2,1)S(1)} %get-tuple-element.8, f32[4096]{0:T(1024)S(1)} %bitcast.210, f32[128]{0:T(128)S(1)} %add_rsqrt_fusion.2), kind=kOutput, calls=%fused_computation.40 | convolution fusion | flops 7522484224 | bytes 62669312 | tf_op jit(solution)/shard_map/dot_general | solution.py:73
  128.6 33.0 %all-reduce.7.cloned.1.call-done = bf16[128,4096]{1,0:T(8,128)(2,1)} async-done(((bf16[128,4096]{1,0:T(8,128)(2,1)}), bf16[128,4096]{1,0:T(8,128)(2,1)}) %all-reduce.7.cloned.1.call-update) | async-done | bytes 1048592 | tf_op jit(solution)/shard_map/psum | solution.py:98
  161.6 1.7 fusion.92
  163.3 2.2 fusion.155
  165.5 0.6 copy-done.2
  166.1 0.5 fusion.158
  166.6 4.7 %fusion.139 = f32[16,8,8,128]{3,1,2,0:T(8,128)S(1)} fusion(bf16[2,4096,1024]{2,1,0:T(8,128)(2,1)} %param.18, bf16[128,4096]{1,0:T(8,128)(2,1)S(1)} %get-tuple-element.6, f32[4096]{0:T(1024)S(1)} %bitcast.208, f32[128]{0:T(128)S(1)} %add_rsqrt_fusion.1), kind=kOutput, calls=%fused_computation.107 | convolution fusion | flops 1076101120 | bytes 9978368 | tf_op jit(solution)/shard_map/dot_general | solution.py:57
  171.4 0.1 reshape.268
  171.5 0.3 subtract_convert_fusion.2
  171.8 0.1 copy.53
  171.9 0.3 subtract_convert_fusion
  172.1 0.2 maximum_bitcast_fusion.1
  172.3 4.8 %fusion.197 = (f32[128,2,4]{2,1,0:T(2,128)S(1)}, f32[128,2,4,64]{3,2,1,0:T(4,128)S(1)}) fusion(bf16[1,128,64,2,128]{4,3,2,1,0:T(2,128)(2,1)} %get-tuple-element.9, bf16[128,2,4,64]{3,2,1,0:T(4,128)(2,1)S(1)} %bitcast.202, bf16[128,2,4,64]{3,2,1,0:T(4,128)(2,1)S(1)} %bitcast.200, pred[128,64]{1,0:T(8,128)(4,1)S(1)} %get-tuple-element.34), kind=kOutput, calls=%fused_computation.179 | convolution fusion | flops 17497088 | bytes 4730880 | tf_op jit(solution)/shard_map/bkgd,bskd->bkgs/dot_general | solution.py:37
  177.1 0.5 fusion.178
  177.6 0.1 copy.47
  177.7 0.1 copy.38
  177.8 0.2 copy.39
  178.0 0.8 fusion.167
  178.8 0.1 copy.40
  178.9 0.2 copy.41
  179.1 0.2 copy.43
  179.2 3.5 %fusion.142 = bf16[128,2,4,128]{3,2,1,0:T(4,128)(2,1)S(1)} fusion(bf16[1,128,64,2,128]{4,3,2,1,0:T(2,128)(2,1)} %get-tuple-element.11, f32[128,2,4,64]{3,2,1,0:T(4,128)S(1)} %get-tuple-element.38, f32[128,2,128]{2,1,0:T(2,128)S(1)} %reshape.269, f32[128,2,4]{2,1,0:T(2,128)S(1)} %copy.43, f32[128,2,4]{2,1,0:T(2,128)S(1)} %copy.41, f32[128,2,4]{2,1,0:T(2,128)S(1)} %copy.39), kind=kOutput, calls=%fused_computation.108 | convolution fusion | flops 17367040 | bytes 4861952 | tf_op jit(solution)/shard_map/bkgs,bskd->bkgd/dot_general | solution.py:46
  182.7 0.2 reshape.260
  182.9 5.6 %fusion.33 = bf16[128,4096]{1,0:T(8,128)(2,1)} fusion(bf16[128,1024]{1,0:T(8,128)(2,1)S(1)} %reshape.260, bf16[2,1024,4096]{2,1,0:T(8,128)(2,1)} %param.21), kind=kOutput, calls=%fused_computation.33 | convolution fusion | flops 1074266112 | bytes 9699328 | tf_op jit(solution)/shard_map/dot_general | solution.py:64
  188.5 0.3 all-reduce.11.cloned.1.call-start
  188.8 0.5 maximum_maximum_fusion
  189.3 32.3 %all-reduce.9.cloned.1.call-done = bf16[128,4096]{1,0:T(8,128)(2,1)} async-done(((bf16[128,4096]{1,0:T(8,128)(2,1)}), bf16[128,4096]{1,0:T(8,128)(2,1)}) %all-reduce.9.cloned.1.call-update) | async-done | bytes 1048592 | tf_op jit(solution)/shard_map/psum | solution.py:96
  221.6 1.7 fusion.95
  223.3 12.7 %fusion.60 = f32[128,3584]{1,0:T(8,128)} fusion(bf16[2,4096,3584]{2,1,0:T(8,128)(2,1)} %param.23, bf16[128,4096]{1,0:T(8,128)(2,1)S(1)} %get-tuple-element.4, f32[4096]{0:T(1024)S(1)} %bitcast.204, f32[128]{0:T(128)S(1)} %add_rsqrt_fusion), kind=kOutput, calls=%fused_computation.42 | convolution fusion | flops 3761111040 | bytes 32260608 | tf_op jit(solution)/shard_map/dot_general | solution.py:70
  236.0 22.1 %fusion.75 = bf16[128,4096]{1,0:T(8,128)(2,1)} fusion(bf16[2,3584,4096]{2,1,0:T(8,128)(2,1)} %param.25, bf16[2,4096,3584]{2,1,0:T(8,128)(2,1)} %param.24, f32[128,3584]{1,0:T(8,128)} %fusion.60, bf16[128,4096]{1,0:T(8,128)(2,1)S(1)} %get-tuple-element.4, f32[4096]{0:T(1024)S(1)} %bitcast.205, f32[128]{0:T(128)S(1)} %add_rsqrt_fusion), kind=kOutput, calls=%fused_computation.47 | convolution fusion | flops 7522484224 | bytes 62669312 | tf_op jit(solution)/shard_map/dot_general | solution.py:73
  258.1 26.6 %broadcast_select_fusion = (bf16[2,128,64,2,128]{4,3,2,1,0:T(2,128)(2,1)}, bf16[2,128,64,2,128]{4,3,2,1,0:T(2,128)(2,1)}) fusion(bf16[2,128,64,2,128]{4,3,2,1,0:T(2,128)(2,1)} %param.16, pred[128,64]{1,0:T(8,128)(4,1)S(1)} %get-tuple-element.33, bf16[2,128,2,128]{3,2,1,0:T(2,128)(2,1)S(1)} %get-tuple-element.40, bf16[2,128,64,2,128]{4,3,2,1,0:T(2,128)(2,1)} %param.15, ...), kind=kLoop, calls=%fused_computation.18 | loop fusion | flops 8388608 | bytes 33824768 | tf_op jit(solution)/shard_map/jit(_where)/select_n | solution.py:78
  284.8 6.4 %all-reduce.11.cloned.1.call-done = bf16[128,4096]{1,0:T(8,128)(2,1)} async-done(((bf16[128,4096]{1,0:T(8,128)(2,1)}), bf16[128,4096]{1,0:T(8,128)(2,1)}) %all-reduce.11.cloned.1.call-update) | async-done | bytes 1048592 | tf_op jit(solution)/shard_map/psum | solution.py:98
  291.2 2.4 add.113
  (25 shorter events, 0.5 us)
Async XLA Ops:
  7.2 84.8 %all-reduce.5.cloned.1.call-start = ((), (), s32[]{:S(2)}) async-start(), calls=%async_computation | async-start | bytes 2097152 | tf_op jit(solution)/shard_map/psum | solution.py:96
  11.0 2.6 copy-start
  50.7 5.9 %copy-start.1 = (bf16[2,4096]{1,0:T(2,128)(2,1)S(1)}, bf16[2,4096]{1,0:T(2,128)(2,1)}, u32[]{:S(2)}) copy-start(bf16[2,4096]{1,0:T(2,128)(2,1)} %param.22) | copy-start | bytes 49156
  56.4 105.2 %all-reduce.7.cloned.1.call-start = ((), (), s32[]{:S(2)}) async-start(), calls=%async_computation.1 | async-start | bytes 2097152 | tf_op jit(solution)/shard_map/psum | solution.py:98
  128.5 93.0 %all-reduce.9.cloned.1.call-start = ((), (), s32[]{:S(2)}) async-start(), calls=%async_computation.2 | async-start | bytes 2097152 | tf_op jit(solution)/shard_map/psum | solution.py:96
  163.3 2.8 copy-start.2
  188.5 102.6 %all-reduce.11.cloned.1.call-start = ((), (), s32[]{:S(2)}) async-start(), calls=%async_computation.3 | async-start | bytes 2097152 | tf_op jit(solution)/shard_map/psum | solution.py:98
Sparse Core Ops, SparseCore 0:
  56.5 35.4 all-reduce.4
  128.7 32.8 all-reduce.6
  188.6 32.8 all-reduce.8
  258.2 32.8 all-reduce.10
where the time goes:
time: 301 us; the launch traced here: 300 us
  matrix products  111 us (37%)
  waiting for transfers between devices  107 us (36%)
  other arithmetic  41.9 us (14%)
  local copies, waits for them, and re-layouts  25.3 us (8%)
  between operations  14.1 us (5%)
    psum x4, waiting for transfers between devices, local_step(): hidden = hidden + lax.psum(part_out, 'tp')  107 us
    dot_general x2, matrix products, mlp_block(): jnp.dot(activated, wd_layer, preferred_element_type=jnp.float32)  44.2 us
    select_n x1, other arithmetic, write_rows(): return jnp.where(at_pos, rows[:, :, None], cache)  26.6 us
    dot_general x2, matrix products, mlp_block(): jnp.dot(normed, wg_layer, preferred_element_type=jnp.float32)  25.5 us
    slice x1, local copies, waits for them, and re-layouts, local_step(): k_cache[layer]  12.1 us
    dot_general x2, matrix products, attention_block(): jnp.dot(attended.reshape(batch_size, q_heads * head_dim), wo_layer, prefe...  11.2 us
    slice x1, local copies, waits for them, and re-layouts, local_step(): v_cache[layer]  10.3 us
    dot_general x2, matrix products, attention_block(): jnp.dot(normed, wq_layer, preferred_element_type=jnp.float32)  9.37 us
  transfers between devices with their start and end apart: 4, of which 4 were waited for; matrix products, arithmetic and copies ran while one was open for 9% of the time, Pallas kernels for 0%

commit v1 on v0

v1 whole, which is shorter than its diff:
```python
import math
import jax
import jax.numpy as jnp
from jax import lax
from jax.experimental import pallas as pl
from jax.experimental.pallas import tpu as pltpu
from jax.sharding import PartitionSpec as P

MESH = pl.DeviceIdType.MESH
F32 = jnp.float32
BF16 = jnp.bfloat16

ROWS = 128
WIDTH = 4096
CHUNK = 512
PIECES = WIDTH // CHUNK
HALF = ROWS // 2
QH = 8
HD = 128
SEQ = 64
KV2 = 2 * SEQ
FFL = 3584
NU = 10
N_Q, N_O, N_G, N_D = 3, 2, 14, 8
PER_LAYER = N_Q + N_O + N_G + N_D
LAYERS = 2
UNITS = LAYERS * PER_LAYER
GROUP = 16


def rope_tables(positions, head_dim):
    half_dim = head_dim // 2
    inv_freq = jnp.power(500000.0, -jnp.arange(half_dim, dtype=jnp.float32) * (2.0 / head_dim))
    wavelen = (2.0 * math.pi) / inv_freq
    smooth = (8192.0 / wavelen - 1.0) / 3.0
    blended = (1.0 - smooth) * inv_freq / 8.0 + smooth * inv_freq
    scaled = jnp.where(wavelen < 2048.0, inv_freq, jnp.where(wavelen > 8192.0, inv_freq / 8.0, blended))
    angles = positions.astype(jnp.float32)[:, None] * scaled[None, :]
    cos_tab, sin_tab = jnp.cos(angles), jnp.sin(angles)
    return jnp.stack([jnp.concatenate([cos_tab, cos_tab], -1), jnp.concatenate([-sin_tab, sin_tab], -1)])


def segments():
    segs = []
    for layer in range(LAYERS):
        base = layer * PER_LAYER
        segs.append(("q", layer, base, base + 2))
        segs.append(("kv", layer, base + 2, base + 3))
        segs.append(("o", layer, base + 3, base + 5))
        segs.append(("g", layer, base + 5, base + 19))
        segs.append(("d", layer, base + 19, base + 27))
    return segs


def layers_kernel(pos_ref, x_hbm, rope_hbm, an_hbm, mn_hbm, kc_hbm, vc_hbm, wq, wk, wv, wo, wg, wu, wd,
                  x_out, kn_out, vn_out,
                  wbuf, kbuf, vbuf, x_ref, h_ref, rope, anorm, mnorm, qbuf, obuf, ob16, knew, vnew, act,
                  part, ra, sb, rb, rc, rd,
                  wsem, csem, lsem, sa_s, sa_r, sb_s, sb_r, sc_s, sc_r, sd_s, sd_r):
    me = lax.axis_index("tp")
    core = lax.rem(me, 2)
    sibling = me + 1 - 2 * core
    across = lax.rem(me + 2, 4)
    mine = pl.ds(pl.multiple_of(core * HALF, HALF), HALF)
    other = pl.ds(pl.multiple_of((1 - core) * HALF, HALF), HALF)
    segs = segments()

    def copies(kind, layer, r, slot):
        col = pl.multiple_of(r * CHUNK, CHUNK) if kind != "g" else pl.multiple_of(r * 256, 256)
        if kind == "q":
            return [(wq.at[layer, :, pl.ds(col, CHUNK)], wbuf.at[slot])]
        if kind == "kv":
            return [(wk.at[layer], wbuf.at[slot, :, pl.ds(0, 256)]), (wv.at[layer], wbuf.at[slot, :, pl.ds(256, 256)])]
        if kind == "o":
            return [(wo.at[layer, :, pl.ds(pl.multiple_of((r * 4 + s) * CHUNK, CHUNK), CHUNK)],
                     wbuf.at[slot, pl.ds(s * 1024, 1024), :]) for s in range(4)]
        if kind == "g":
            return [(wg.at[layer, :, pl.ds(col, 256)], wbuf.at[slot, :, pl.ds(0, 256)]),
                    (wu.at[layer, :, pl.ds(col, 256)], wbuf.at[slot, :, pl.ds(256, 256)])]
        return [(wd.at[layer, :, pl.ds(col, CHUNK)], wbuf.at[slot, pl.ds(0, FFL), :])]

    def issue(t, lo, hi):
        for kind, layer, s, e in segs:
            if e <= lo or s >= hi:
                continue

            def go(kind=kind, layer=layer, s=s):
                slot = lax.rem(t, NU)
                for src, dst in copies(kind, layer, t - s, slot):
                    pltpu.make_async_copy(src, dst, wsem.at[slot]).start()

            if s <= lo and hi <= e:
                go()
            else:
                pl.when((t >= s) & (t < e))(go)

    def wait_unit(slot, down=False):
        if down:
            src, dst = wd.at[0, :, pl.ds(0, CHUNK)], wbuf.at[slot, pl.ds(0, FFL), :]
        else:
            src, dst = wq.at[0, :, pl.ds(0, CHUNK)], wbuf.at[slot]
        pltpu.make_async_copy(src, dst, wsem.at[slot]).wait()

    def cache_copies(layer):
        return [pltpu.make_async_copy(kc_hbm.at[layer], kbuf, csem.at[0]),
                pltpu.make_async_copy(vc_hbm.at[layer], vbuf, csem.at[1])]

    small = [pltpu.make_async_copy(x_hbm, x_ref, lsem.at[0]), pltpu.make_async_copy(an_hbm, anorm, lsem.at[1]),
             pltpu.make_async_copy(rope_hbm, rope, lsem.at[2]), pltpu.make_async_copy(mn_hbm, mnorm, lsem.at[3])]
    for c in small:
        c.start()
    for t in range(3):
        issue(jnp.int32(t), t, t + 1)
    for c in cache_copies(0):
        c.start()
    for t in range(3, NU):
        issue(jnp.int32(t), t, t + 1)

    barrier = pltpu.get_barrier_semaphore()
    for dev in (sibling, across):
        pl.semaphore_signal(barrier, inc=1, device_id={"tp": dev}, device_id_type=MESH)
    pl.semaphore_wait(barrier, 2)
    small[0].wait()
    small[1].wait()

    def lanes(j, n):
        return pl.ds(pl.multiple_of(j * n, n), n)

    def sum_sq(v):
        sq = v * v
        acc = sq[:, 0:128]
        for k in range(1, v.shape[1] // 128):
            acc = acc + sq[:, k * 128:(k + 1) * 128]
        return acc

    def normalize(acc, norm, layer):
        mean_sq = jnp.sum(acc, axis=-1, keepdims=True) * (1.0 / WIDTH)
        scale = lax.rsqrt(mean_sq + 1e-5)

        def body(j, carry):
            w = norm[:, lanes(j, CHUNK)].astype(F32)[layer:layer + 1, :]
            xv = x_ref[:, lanes(j, CHUNK)].astype(F32)
            h_ref[:, lanes(j, CHUNK)] = (xv * scale * w).astype(BF16)
            return carry

        lax.fori_loop(0, PIECES, body, 0)

    def remote(src, dst, send, recv, dev):
        return pltpu.make_async_remote_copy(src_ref=src, dst_ref=dst, send_sem=send, recv_sem=recv,
                                            device_id={"tp": dev}, device_id_type=MESH)

    def copy_a(p, j):
        return remote(part.at[j, other, :], ra.at[p, j], sa_s.at[j], sa_r.at[p, j], sibling)

    def copy_b(p, j):
        return remote(sb.at[j], rb.at[p, j], sb_s.at[j], sb_r.at[p, j], across)

    def copy_c(p, j):
        return remote(sb.at[j], rc.at[p, j], sc_s.at[j], sc_r.at[p, j], sibling)

    def copy_d(p, j):
        return remote(rb.at[p, j], rd.at[p, j], sd_s.at[j], sd_r.at[p, j], sibling)

    def stage_a(p, j):
        copy_a(p, j).wait_recv()
        total = part[j, mine, :].astype(F32) + ra[p, j].astype(F32)
        sb[j] = total.astype(BF16)
        copy_b(p, j).start()
        copy_c(p, j).start()

    def finish(p, lag):
        for j in range(PIECES - lag, PIECES):
            stage_a(p, j)

        def add(j):
            cols = lanes(j, CHUNK)
            near = (sb[j].astype(F32) + rb[p, j].astype(F32)).astype(BF16).astype(F32)
            new = (x_ref[mine, cols].astype(F32) + near).astype(BF16)
            x_ref[mine, cols] = new
            copy_c(p, j).wait_recv()
            copy_d(p, j).wait_recv()
            far = (rc[p, j].astype(F32) + rd[p, j].astype(F32)).astype(BF16).astype(F32)
            new = (x_ref[other, cols].astype(F32) + far).astype(BF16)
            x_ref[other, cols] = new
            copy_a(p, j).wait_send()
            copy_b(p, j).wait_send()
            copy_c(p, j).wait_send()
            copy_d(p, j).wait_send()
            return sum_sq(x_ref[:, cols].astype(F32))

        def forward(j):
            copy_b(p, j).wait_recv()
            copy_d(p, j).start()

        forward(0)

        def body(j, acc):
            forward(j)
            return acc + add(j - 1)

        acc = lax.fori_loop(1, PIECES, body, jnp.zeros((ROWS, 128), F32))
        return acc + add(PIECES - 1)

    row_id = lax.broadcasted_iota(jnp.int32, (16, 256), 0)
    col_id = lax.broadcasted_iota(jnp.int32, (16, 256), 1)
    fits = ((row_id // 8) == (col_id // KV2)) & (((row_id % 8) // 4) == (col_id % 2))
    limit = jnp.where(fits, (col_id % KV2) // 2, 1 << 20)
    first_req = col_id < KV2
    pair_row = (lax.broadcasted_iota(jnp.int32, (KV2, HD), 0) // 2).astype(F32).astype(BF16)
    odd = (lax.broadcasted_iota(jnp.int32, (16, HD), 0) % 2) == 1

    def with_new(buf, new, b, pos):
        old = buf[pl.ds(pl.multiple_of(b * KV2, KV2), KV2), :]
        tile = jnp.where(odd, new[1:2, :], new[0:1, :]).astype(BF16)
        fresh = jnp.concatenate([tile] * (KV2 // 16), axis=0)
        here = pair_row == jnp.full((KV2, HD), pos.astype(F32), F32).astype(BF16)
        return jnp.where(here, fresh, old)

    def attention():
        def body(g, carry):
            kn = knew[pl.ds(pl.multiple_of(g * 2 * GROUP, 2 * GROUP), 2 * GROUP), :]
            vn = vnew[pl.ds(pl.multiple_of(g * 2 * GROUP, 2 * GROUP), 2 * GROUP), :]
            for pr in range(GROUP // 2):
                b0 = g * GROUP + 2 * pr
                p0, p1 = pos_ref[b0], pos_ref[b0 + 1]
                at = 4 * pr
                kk = jnp.concatenate([with_new(kbuf, kn[at:at + 2], b0, p0), with_new(kbuf, kn[at + 2:at + 4], b0 + 1, p1)], axis=0)
                vv = jnp.concatenate([with_new(vbuf, vn[at:at + 2], b0, p0), with_new(vbuf, vn[at + 2:at + 4], b0 + 1, p1)], axis=0)
                q2 = qbuf[pl.ds(pl.multiple_of(b0 * QH, 16), 16), :].astype(BF16)
                sc = lax.dot_general(q2, kk, (((1,), (1,)), ((), ())), preferred_element_type=F32) * (HD ** -0.5)
                sc = jnp.where(limit <= jnp.where(first_req, p0, p1), sc, -jnp.inf)
                ex = jnp.exp(sc - jnp.max(sc, axis=-1, keepdims=True))
                prob = (ex * (1.0 / jnp.sum(ex, axis=-1, keepdims=True))).astype(BF16)
                o = jnp.dot(prob, vv, preferred_element_type=F32)
                obuf[pl.ds(pl.multiple_of(b0 * QH, 16), 16), :] = o
            return carry

        lax.fori_loop(0, ROWS // GROUP, body, 0)
        for j in range(QH):
            ob16[:, j * HD:(j + 1) * HD] = obuf[pl.ds(j, ROWS, stride=QH), :].astype(BF16)

    def first_sq(j, acc):
        return acc + sum_sq(x_ref[:, lanes(j, CHUNK)].astype(F32))

    acc = lax.fori_loop(0, PIECES, first_sq, jnp.zeros((ROWS, 128), F32))
    for layer in range(LAYERS):
        base = layer * PER_LAYER
        normalize(acc, anorm, layer)
        if layer == 0:
            small[2].wait()
            small[3].wait()

        for i in range(N_Q):
            t = base + i
            slot = t % NU
            wait_unit(slot)
            res = jnp.dot(h_ref[...], wbuf[slot], preferred_element_type=F32).astype(BF16).astype(F32)
            if t + NU < UNITS:
                issue(jnp.int32(t + NU), t + NU, t + NU + 1)
            for hh in range(CHUNK // HD):
                v = res[:, hh * HD:(hh + 1) * HD]
                if i < 2 or hh < 2:
                    v = v * rope[0] + pltpu.roll(v, HD // 2, 1) * rope[1]
                    v = v.astype(BF16).astype(F32)
                if i < 2:
                    qbuf[pl.ds(i * 4 + hh, ROWS, stride=QH), :] = v
                elif hh < 2:
                    knew[pl.ds(hh, ROWS, stride=2), :] = v
                else:
                    vnew[pl.ds(hh - 2, ROWS, stride=2), :] = v
        kn_out[layer] = knew[...].astype(BF16)
        vn_out[layer] = vnew[...].astype(BF16)

        for c in cache_copies(layer):
            c.wait()
        attention()
        if layer + 1 < LAYERS:
            for c in cache_copies(layer + 1):
                c.start()

        p = 0
        lag_o = 4
        for u in range(N_O):
            t = base + N_Q + u
            slot = t % NU
            wait_unit(slot)

            def out_piece(s, carry, u=u, slot=slot):
                j = u * 4 + s
                w = wbuf[slot, pl.ds(pl.multiple_of(s * 1024, 1024), 1024), :]
                part[j] = jnp.dot(ob16[...], w, preferred_element_type=F32).astype(BF16)
                copy_a(p, j).start()

                @pl.when(j >= lag_o)
                def _():
                    stage_a(p, j - lag_o)

                return carry

            lax.fori_loop(0, 4, out_piece, 0)
            if t + NU < UNITS:
                issue(jnp.int32(t + NU), t + NU, t + NU + 1)
        acc = finish(p, lag_o)
        normalize(acc, mnorm, layer)

        def gate_up(i, carry):
            t = base + N_Q + N_O + i
            slot = lax.rem(t, NU)
            wait_unit(slot)
            res = jnp.dot(h_ref[...], wbuf[slot], preferred_element_type=F32).astype(BF16).astype(F32)
            lo = base + N_Q + N_O + NU

            if lo + N_G <= UNITS:
                issue(t + NU, lo, lo + N_G)
            else:
                issue(t + NU, lo, UNITS)
            gate, up = res[:, :256], res[:, 256:]
            act[:, lanes(i, 256)] = (gate * (1.0 / (1.0 + jnp.exp(-gate))) * up).astype(BF16)
            return carry

        lax.fori_loop(0, N_G, gate_up, 0)

        p = 1
        lag_d = 2

        def down_piece(j, carry):
            t = base + N_Q + N_O + N_G + j
            slot = lax.rem(t, NU)
            wait_unit(slot, down=True)
            part[j] = jnp.dot(act[...], wbuf[slot, pl.ds(0, FFL), :], preferred_element_type=F32).astype(BF16)
            copy_a(p, j).start()
            lo = base + N_Q + N_O + N_G + NU
            if lo < UNITS:
                issue(t + NU, lo, min(lo + N_D, UNITS))

            @pl.when(j >= lag_d)
            def _():
                stage_a(p, j - lag_d)

            return carry

        lax.fori_loop(0, N_D, down_piece, 0)
        acc = finish(p, lag_d)

    x_out[...] = x_ref[...]


def run_layers(positions, hidden, rope, attn_norm, mlp_norm, kc, vc, wq, wk, wv, wo, wg, wu, wd):
    any_spec = pl.BlockSpec(memory_space=pl.ANY)
    vmem = pl.BlockSpec(memory_space=pltpu.VMEM)
    dma = pltpu.SemaphoreType.DMA
    piece = (PIECES, HALF, CHUNK)
    return pl.pallas_call(
        layers_kernel,
        name="layers",
        out_shape=(jax.ShapeDtypeStruct((ROWS, WIDTH), BF16),
                   jax.ShapeDtypeStruct((LAYERS, 2 * ROWS, HD), BF16),
                   jax.ShapeDtypeStruct((LAYERS, 2 * ROWS, HD), BF16)),
        in_specs=[pl.BlockSpec(memory_space=pltpu.SMEM)] + [any_spec] * 13,
        out_specs=(vmem, vmem, vmem),
        scratch_shapes=[
            pltpu.VMEM((NU, WIDTH, CHUNK), BF16),
            pltpu.VMEM((ROWS * KV2, HD), BF16),
            pltpu.VMEM((ROWS * KV2, HD), BF16),
            pltpu.VMEM((ROWS, WIDTH), BF16),
            pltpu.VMEM((ROWS, WIDTH), BF16),
            pltpu.VMEM((2, ROWS, HD), F32),
            pltpu.VMEM((LAYERS, WIDTH), BF16),
            pltpu.VMEM((LAYERS, WIDTH), BF16),
            pltpu.VMEM((ROWS * QH, HD), F32),
            pltpu.VMEM((ROWS * QH, HD), F32),
            pltpu.VMEM((ROWS, QH * HD), BF16),
            pltpu.VMEM((2 * ROWS, HD), F32),
            pltpu.VMEM((2 * ROWS, HD), F32),
            pltpu.VMEM((ROWS, FFL), BF16),
            pltpu.VMEM((PIECES, ROWS, CHUNK), BF16),
            pltpu.VMEM((2,) + piece, BF16),
            pltpu.VMEM(piece, BF16),
            pltpu.VMEM((2,) + piece, BF16),
            pltpu.VMEM((2,) + piece, BF16),
            pltpu.VMEM((2,) + piece, BF16),
            dma((NU,)), dma((2,)), dma((4,)),
            dma((PIECES,)), dma((2, PIECES)), dma((PIECES,)), dma((2, PIECES)),
            dma((PIECES,)), dma((2, PIECES)), dma((PIECES,)), dma((2, PIECES)),
        ],
        compiler_params=pltpu.CompilerParams(collective_id=0, has_side_effects=True, vmem_limit_bytes=67043328),
    )(positions, hidden, rope, attn_norm, mlp_norm, kc, vc, wq, wk, wv, wo, wg, wu, wd)


BLOCK = 32
CACHE_BLOCKS = LAYERS * ROWS // BLOCK


def cache_kernel(pos_ref, kc, vc, kn, vn, ko, vo, buf, isem, osem):
    where = [(which, layer, b) for layer in range(LAYERS) for b in range(0, ROWS, BLOCK) for which in range(2)]
    ins, outs = [], []
    for n, (which, layer, b) in enumerate(where):
        ins.append(pltpu.make_async_copy((kc, vc)[which].at[layer, pl.ds(b, BLOCK)], buf.at[n], isem.at[n]))
        outs.append(pltpu.make_async_copy(buf.at[n], (ko, vo)[which].at[layer, pl.ds(b, BLOCK)], osem.at[n]))
    for c in ins:
        c.start()
    for n, (which, layer, b) in enumerate(where):
        ins[n].wait()
        new = (kn, vn)[which]

        def row(i, carry, n=n, layer=layer, b=b, new=new):
            buf[n, i, pos_ref[b + i]] = new[layer, b + i]
            return carry

        lax.fori_loop(0, BLOCK, row, 0, unroll=8)
        outs[n].start()
    for c in outs:
        c.wait()


def write_cache(positions, k_cache, v_cache, k_new, v_new):
    any_spec = pl.BlockSpec(memory_space=pl.ANY)
    vmem = pl.BlockSpec(memory_space=pltpu.VMEM)
    return pl.pallas_call(
        cache_kernel,
        name="cache",
        out_shape=(jax.ShapeDtypeStruct(k_cache.shape, BF16), jax.ShapeDtypeStruct(v_cache.shape, BF16)),
        in_specs=[pl.BlockSpec(memory_space=pltpu.SMEM), any_spec, any_spec, vmem, vmem],
        out_specs=(any_spec, any_spec),
        scratch_shapes=[pltpu.VMEM((2 * CACHE_BLOCKS, BLOCK, SEQ, 2, HD), BF16),
                        pltpu.SemaphoreType.DMA((2 * CACHE_BLOCKS,)), pltpu.SemaphoreType.DMA((2 * CACHE_BLOCKS,))],
        compiler_params=pltpu.CompilerParams(vmem_limit_bytes=67043328),
    )(positions, k_cache, v_cache, k_new, v_new)


def solution(mesh):
    row_spec = P('dp', None)
    pos_spec = P('dp')
    cache_spec = P(None, 'dp', None, 'tp', None)
    norm_spec = P(None, None)
    col_spec = P(None, None, 'tp')
    split_rows = P(None, 'tp', None)

    def local_step(hidden, positions, k_cache, v_cache, attn_norm, w_query, w_key, w_value, w_out, mlp_norm, w_gate, w_up, w_down):
        rope = rope_tables(positions, HD)
        flat = (LAYERS, ROWS * KV2, HD)
        x, k_new, v_new = run_layers(positions, hidden, rope, attn_norm, mlp_norm, k_cache.reshape(flat), v_cache.reshape(flat),
                                     w_query, w_key, w_value, w_out, w_gate, w_up, w_down)
        pair = (LAYERS, ROWS, 2, HD)
        k_out, v_out = write_cache(positions, k_cache, v_cache, k_new.reshape(pair), v_new.reshape(pair))
        return x, k_out, v_out

    return jax.shard_map(local_step, mesh=mesh, in_specs=(row_spec, pos_spec, cache_spec, cache_spec, norm_spec, col_spec, col_spec, col_spec, split_rows, norm_spec, col_spec, col_spec, split_rows), out_specs=(row_spec, cache_spec, cache_spec), check_vma=False)
```

time: 301 us -> 170 us (0.56)
  Pallas kernels: 0 us -> 165 us
  matrix products: 111 us -> 0 us
  waiting for transfers between devices: 107 us -> 0 us
  other arithmetic: 41.9 us -> 1.77 us
  local copies, waits for them, and re-layouts: 25.3 us -> 2.29 us
  between operations: 14.1 us -> 0.66 us
    pallas_call x0 -> x2, Pallas kernels: none -> 165 us  [the longest x1 152 us: run_layers(): pl.pallas_call(layers_kernel, name='layers', out_shape=(jax.ShapeDtypeStr...]
    dot_general x18 -> x0, matrix products: 111 us -> none  [the longest x2 44.2 us: mlp_block(): jnp.dot(activated, wd_layer, preferred_element_type=jnp.float32)]
    psum x4 -> x0, waiting for transfers between devices: 107 us -> none  [local_step(): hidden = hidden + lax.psum(part_out, 'tp')]
    select_n x1 -> x0, other arithmetic: 26.6 us -> none  [write_rows(): return jnp.where(at_pos, rows[:, :, None], cache)]
    slice x2 -> x0, local copies, waits for them, and re-layouts: 22.4 us -> none  [the longest x1 12.1 us: local_step(): k_cache[layer]]
    reduce_sum x6 -> x0, other arithmetic: 8.15 us -> none  [the longest x4 6.55 us: rms_norm(): mean_sq = jnp.mean(hidden_f32 * hidden_f32, axis=-1, keepdims=True)]
  transfers between devices with their start and end apart: 4 -> 0, of which waited for: 4 -> 0; matrix products, arithmetic and copies ran while one was open for 9% -> 0% of each run, Pallas kernels for 0% -> 0%
where the time goes in v1:
time: 170 us
  Pallas kernels  165 us (97%)
  local copies, waits for them, and re-layouts  2.29 us (1%)
  other arithmetic  1.77 us (1%)
    pallas_call x1, Pallas kernels, run_layers(): pl.pallas_call(layers_kernel, name='layers', out_shape=(jax.ShapeDtypeStr...  152 us
    pallas_call x1, Pallas kernels, write_cache(): pl.pallas_call(cache_kernel, name='cache', out_shape=(jax.ShapeDtypeStruc...  13 us

profile of v1, /device:TPU:0, one launch (start us, length us, event | category | flops | bytes accessed | tf_op | source)
XLA Modules:
  0.0 169.7 jit_solution(12803727176407339215)
XLA Ops:
  0.6 0.7 convert_element_type.3
  1.3 0.3 multiply_cosine_fusion
  1.6 0.1 maximum_bitcast_fusion
  1.7 0.7 pad_maximum_fusion.rope_hbm
  2.4 151.9 %layers.1 = (bf16[128,4096]{1,0:T(8,128)(2,1)}, bf16[2,256,128]{2,1,0:T(8,128)(2,1)}, bf16[2,256,128]{2,1,0:T(8,128)(2,1)}) custom-call(s32[128]{0:T(128)} %pos_ref.3, bf16[128,4096]{1,0:T(8,128)(2,1)} %x_hbm.1, f32[2,128,128]{2,1,0:T(8,128)} %pad_maximum_fusion.rope_hbm, bf16[2,4096]{1,0:T(2,128)(2,1)} %an_hbm.1, bf16[2,4096]{1,0:T(2,128)(2,1)} %mn_hbm.1, ...), custom_call_target="tpu_custom_call" | custom-call | tf_op jit(solution)/shard_map/layers/pallas_call | solution.py:353
  154.3 13.0 %cache.1 = (bf16[2,128,64,2,128]{4,3,2,1,0:T(2,128)(2,1)}, bf16[2,128,64,2,128]{4,3,2,1,0:T(2,128)(2,1)}) custom-call(s32[128]{0:T(128)} %pos_ref.3, bf16[2,128,64,2,128]{4,3,2,1,0:T(2,128)(2,1)} %kc.1, bf16[2,128,64,2,128]{4,3,2,1,0:T(2,128)(2,1)} %vc.1, bf16[2,128,2,128]{3,2,1,0:T(2,128)(2,1)} %bitcast.10, bf16[2,128,2,128]{3,2,1,0:T(2,128)(2,1)} %bitcast.11), custom_call_target="tpu_custom_call" | custom-call | tf_op jit(solution)/shard_map/cache/pallas_call | solution.py:419
  167.4 2.3 %copy.17 = bf16[128,4096]{1,0:T(8,128)(2,1)} copy(bf16[128,4096]{1,0:T(8,128)(2,1)} %get-tuple-element.21) | data formatting | bytes 2097152
  (1 shorter events, 0.0 us)
